TPU v7x, 32 devices: a whole 2x2x4 slice. The times are simulated.
32 devices in a mesh: section: 4 (over z), seq: 8 (over y, x, core).
Axes of the slice: x: 2, y: 2, z: 4, core: 2. Of those that a mesh axis runs over, the one named last changes fastest.
Arguments:
- saved: bfloat16 [4, 3, 1024, 2304], P('section', None, 'seq'), may hold values from -8 to 8
- cotangent: bfloat16 [3, 1024, 2304], P(None, 'seq'), may hold values from -0.109375 to 0.109375
- slot_table: int32 [4, 3], P('section'), may hold values from 0 to 2, each once within a row
- gain: float32 [4, 2304], P('section'), may hold values from 0.25 to 1.75
- value_weight: bfloat16 [4, 2304, 1024], P('section'), may hold values from -0.125 to 0.125
- out_weight: bfloat16 [4, 2304, 1024], P('section'), may hold values from -0.1875 to 0.1875
Outputs:
- value_grad: float32 [4, 2304, 1024], P('section', 'seq')
- out_grad: float32 [4, 2304, 1024], P('section', 'seq')
- gain_grad: float32 [4, 2304], P('section')
Inputs may be any that keep to these rules, and one draw needn't show every extreme that they name: `slot_table`: each row names every stash slot once.
All inputs are finite; a program needn't handle non-finite values.
Results may differ from a plain program's by a relative error of at most 0.007.
Values may be sent and summed in bfloat16 or wider, within the bound.
A program may use at most 128 MiB of HBM per device.

v0:
```python
import jax
import jax.numpy as jnp
from jax import lax
from jax.sharding import PartitionSpec as P

EPSILON = 1e-06


def passed_along(value, axis, steps):
    count = lax.axis_size(axis)
    first, last = (max(0, -steps), min(count, count - steps))
    return lax.ppermute(value, axis, [(source, source + steps) for source in range(first, last)])


def normalize(inputs, gain_row):
    value_rows = inputs.astype(jnp.float32)
    inv_rms = lax.rsqrt(jnp.mean(value_rows * value_rows, axis=-1, keepdims=True) + EPSILON)
    unit_rows = value_rows * inv_rms
    return (unit_rows, inv_rms, (unit_rows * gain_row).astype(jnp.bfloat16))


def input_grads(inputs, grad_out, gain_row, w_value, w_out):
    unit_rows, inv_rms, normed = normalize(inputs, gain_row)
    grad_value = jnp.dot(grad_out, w_out, preferred_element_type=jnp.float32).astype(jnp.bfloat16)
    grad_normed = lax.dot_general(
        grad_value, w_value, (((1,), (1,)), ((), ())), preferred_element_type=jnp.float32
    )
    gain_term = jnp.sum(grad_normed * unit_rows, axis=0)
    grad_unit = grad_normed * gain_row
    grad_in = grad_out.astype(jnp.float32) + inv_rms * (
        grad_unit - unit_rows * jnp.mean(grad_unit * unit_rows, axis=-1, keepdims=True)
    )
    return (grad_in.astype(jnp.bfloat16), grad_value, normed, gain_term)


def arrivals(
    step_index, sent, section_count, section_index, micro_count, cotangent, local_saved, slot_order
):
    if step_index > 0:
        incoming = passed_along(sent, "section", -1)
    else:
        incoming = sent
    micro_index = step_index - (section_count - 1 - section_index)
    active_now = jnp.logical_and(micro_index >= 0, micro_index < micro_count)
    clipped = jnp.clip(micro_index, 0, micro_count - 1)
    top_grad = lax.dynamic_index_in_dim(cotangent, clipped, 0, keepdims=False)
    grad_out = jnp.where(section_index == section_count - 1, top_grad, incoming)
    slot_index = lax.dynamic_index_in_dim(slot_order, clipped, 0, keepdims=False)
    inputs = lax.dynamic_index_in_dim(local_saved, slot_index, 0, keepdims=False)
    return (active_now, clipped, grad_out, inputs)


def per_device(saved, cotangent, slot_table, gain, value_weight, out_weight):
    section_count = lax.axis_size("section")
    section_index = lax.axis_index("section")
    micro_count = slot_table.shape[1]
    local_saved = saved[0]
    slot_order = slot_table[0]
    gain_row = gain[0]
    w_value = value_weight[0]
    w_out = out_weight[0]
    token_rows = cotangent.shape[1]
    model_width = w_value.shape[0]
    inner_width = w_value.shape[1]
    sent = jnp.zeros((token_rows, model_width), jnp.bfloat16)
    gain_acc = jnp.zeros((model_width,), jnp.float32)
    out_stash = jnp.zeros((micro_count, token_rows, model_width), jnp.bfloat16)
    value_stash = jnp.zeros((micro_count, token_rows, inner_width), jnp.bfloat16)
    for step_index in range(micro_count + section_count - 1):
        active_now, clipped, grad_out, inputs = arrivals(
            step_index,
            sent,
            section_count,
            section_index,
            micro_count,
            cotangent,
            local_saved,
            slot_order,
        )

        def working(carried):
            grad_in, grad_value, normed, gain_term = input_grads(
                inputs, grad_out, gain_row, w_value, w_out
            )
            new_out = lax.dynamic_update_index_in_dim(carried[2], grad_out, clipped, 0)
            new_value = lax.dynamic_update_index_in_dim(carried[3], grad_value, clipped, 0)
            return (grad_in, carried[1] + gain_term, new_out, new_value)

        def resting(carried):
            return carried

        sent, gain_acc, out_stash, value_stash = lax.cond(
            active_now, working, resting, (sent, gain_acc, out_stash, value_stash)
        )
    ordered = jnp.take(local_saved, slot_order, axis=0).reshape(
        micro_count * token_rows, model_width
    )
    unit_all, inv_all, normed_all = normalize(ordered, gain_row)
    values_all = jnp.dot(normed_all, w_value, preferred_element_type=jnp.float32).astype(
        jnp.bfloat16
    )
    grads_all = out_stash.reshape(micro_count * token_rows, model_width)
    grad_values = value_stash.reshape(micro_count * token_rows, inner_width)
    value_acc = lax.dot_general(
        normed_all, grad_values, (((0,), (0,)), ((), ())), preferred_element_type=jnp.float32
    )
    out_acc = lax.dot_general(
        grads_all, values_all, (((0,), (0,)), ((), ())), preferred_element_type=jnp.float32
    )
    value_grad, out_grad = (
        lax.psum_scatter(value_acc, "seq", scatter_dimension=0, tiled=True),
        lax.psum_scatter(out_acc, "seq", scatter_dimension=0, tiled=True),
    )
    gain_total = lax.psum(gain_acc, "seq")
    return (value_grad[None], out_grad[None], gain_total[None])


def solution(mesh):
    in_specs = (
        P("section", None, "seq", None),
        P(None, "seq", None),
        P("section", None),
        P("section", None),
        P("section", None, None),
        P("section", None, None),
    )
    out_specs = (P("section", "seq", None), P("section", "seq", None), P("section", None))
    return jax.shard_map(
        per_device, mesh=mesh, in_specs=in_specs, out_specs=out_specs, check_vma=False
    )
```

profile of v0, /device:TPU:0, one launch (start us, length us, event | category | flops | bytes accessed | tf_op | source)
XLA Modules:
  0.0 357.3 jit_solution(471930635326041545)
XLA Ops:
  7.2 1.5 constant_dynamic-slice_fusion.2
  17.5 3.1 dynamic-slice_bitcast_fusion
  20.6 3.2 conditional.6
  20.6 1.3 broadcast_in_dim.72
  23.7 1.3 collective-permute-start
  25.0 17.1 %collective-permute-done = bf16[128,2304]{1,0:T(8,128)(2,1)} collective-permute-done((bf16[128,2304]{1,0:T(8,128)(2,1)}, bf16[128,2304]{1,0:T(8,128)(2,1)}, u32[]{:S(2)}, u32[]{:S(2)}) %collective-permute-start) | collective-permute-done | bytes 589856 | tf_op jit(solution)/shard_map/ppermute | solution.py:12
  43.3 1.3 collective-permute-start.1
  44.6 15.4 %collective-permute-done.1 = bf16[128,2304]{1,0:T(8,128)(2,1)} collective-permute-done((bf16[128,2304]{1,0:T(8,128)(2,1)}, bf16[128,2304]{1,0:T(8,128)(2,1)}, u32[]{:S(2)}, u32[]{:S(2)}) %collective-permute-start.1) | collective-permute-done | bytes 589856 | tf_op jit(solution)/shard_map/ppermute | solution.py:12
  61.1 1.3 collective-permute-start.2
  62.5 1.3 reduce.6
  64.8 46.2 %collective-permute-done.2 = bf16[128,2304]{1,0:T(8,128)(2,1)S(1)} collective-permute-done((bf16[128,2304]{1,0:T(8,128)(2,1)}, bf16[128,2304]{1,0:T(8,128)(2,1)S(1)}, u32[]{:S(2)}, u32[]{:S(2)}) %collective-permute-start.2) | collective-permute-done | bytes 589856 | tf_op jit(solution)/shard_map/ppermute | solution.py:12
  111.2 10.7 %conditional.9 = ((bf16[128,2304]{1,0:T(8,128)(2,1)}, f32[2304]{0:T(1024)S(1)}, bf16[3,128,2304]{2,1,0:T(8,128)(2,1)}, bf16[3,128,1024]{2,1,0:T(8,128)(2,1)})) conditional(s32[]{:T(128)} %convert_element_type.128, (bf16[128,2304]{1,0:T(8,128)(2,1)}, f32[2304]{0:T(1024)S(1)}, bf16[3,128,2304]{2,1,0:T(8,128)(2,1)}, ...), branch_computations={%region_16.17_spmd, %region_17.21_spmd} | conditional | flops 1213694080 | bytes 17416818 | solution.py:92
  111.4 3.9 %bitcast_dynamic-update-slice_fusion.9 = (bf16[3,128,1024]{2,1,0:T(8,128)(2,1)}, bf16[128,1024]{1,0:T(8,128)(2,1)S(1)}) fusion(bf16[3,128,1024]{2,1,0:T(8,128)(2,1)} %get-tuple-element.287, s32[]{:T(128)S(6)} %select_n.110, bf16[128,2304]{1,0:T(8,128)(2,1)S(1)} %get-tuple-element.279, bf16[2304,1024]{1,0:T(8,128)(2,1)} %get-tuple-element.281), kind=kOutput, calls=%fused_computation.78 | convolution fusion | flops 604110848 | bytes 5832708 | tf_op jit(solution)/shard_map/cond/branch_1_fun/dot_general | solution.py:24
  115.6 4.2 %fusion.41 = (f32[2304]{0:T(1024)S(1)}, f32[128]{0:T(128)S(1)}, f32[128,2304]{1,0:T(8,128)S(1)}) fusion(bf16[128,2304]{1,0:T(8,128)(2,1)S(1)} %get-tuple-element.280, f32[128]{0:T(128)S(1)} %add_rsqrt_fusion.4, f32[2304]{0:T(1024)S(1)} %reduce.4, bf16[128,1024]{1,0:T(8,128)(2,1)S(1)} %get-tuple-element.495, bf16[2304,1024]{1,0:T(8,128)(2,1)} %get-tuple-element.282), kind=kOutput, calls=%fused_computation.75 | convolution fusion | flops 606041728 | bytes 6769664 | tf_op jit(solution)/shard_map/cond/branch_1_fun/dot_general | solution.py:25
  121.9 1.3 collective-permute-start.3
  125.1 12.3 %collective-permute-done.3 = bf16[128,2304]{1,0:T(8,128)(2,1)} collective-permute-done((bf16[128,2304]{1,0:T(8,128)(2,1)}, bf16[128,2304]{1,0:T(8,128)(2,1)}, u32[]{:S(2)}, u32[]{:S(2)}) %collective-permute-start.3) | collective-permute-done | bytes 589856 | tf_op jit(solution)/shard_map/ppermute | solution.py:12
  138.2 16.7 %conditional.10 = ((bf16[128,2304]{1,0:T(8,128)(2,1)}, f32[2304]{0:T(1024)S(1)}, bf16[3,128,2304]{2,1,0:T(8,128)(2,1)}, bf16[3,128,1024]{2,1,0:T(8,128)(2,1)})) conditional(s32[]{:T(128)} %convert_element_type.127, (bf16[128,2304]{1,0:T(8,128)(2,1)}, f32[2304]{0:T(1024)S(1)}, bf16[3,128,2304]{2,1,0:T(8,128)(2,1)}, ...), branch_computations={%region_21.22_spmd, %region_22.26_spmd.clone.clone} | conditional | flops 1213988992 | bytes 23612748 | solution.py:92
  138.2 2.3 bitcast_dynamic-update-slice_fusion.10
  140.6 4.2 %bitcast_dynamic-update-slice_fusion.11 = (bf16[3,128,1024]{2,1,0:T(8,128)(2,1)}, bf16[128,1024]{1,0:T(8,128)(2,1)}) fusion(bf16[3,128,1024]{2,1,0:T(8,128)(2,1)} %get-tuple-element.434, s32[]{:T(128)S(6)} %select_n.153, bf16[128,2304]{1,0:T(8,128)(2,1)S(1)} %get-tuple-element.481, bf16[2304,1024]{1,0:T(8,128)(2,1)} %get-tuple-element.429), kind=kOutput, calls=%fused_computation.96 | convolution fusion | flops 604110848 | bytes 5832708 | tf_op jit(solution)/shard_map/cond/branch_1_fun/dot_general | solution.py:24
  148.0 1.3 reduce.5
  149.3 4.3 %fusion.51 = (f32[2304]{0:T(1024)S(1)}, f32[128]{0:T(128)S(1)}, f32[128,2304]{1,0:T(8,128)S(1)}) fusion(f32[128]{0:T(128)} %add_rsqrt_fusion.5, bf16[1,3,128,2304]{3,2,1,0:T(8,128)(2,1)S(1)} %get-tuple-element.428, s32[]{:T(128)S(6)} %select_n.152, f32[2304]{0:T(1024)} %reduce.5, bf16[128,1024]{1,0:T(8,128)(2,1)} %get-tuple-element.498, ...), kind=kOutput, calls=%fused_computation.92 | convolution fusion | flops 606041728 | bytes 6769668 | tf_op jit(solution)/shard_map/cond/branch_1_fun/dot_general | solution.py:25
  156.2 2.5 fusion.55
  158.7 10.9 %collective-permute-done.4 = bf16[128,2304]{1,0:T(8,128)(2,1)} collective-permute-done((bf16[128,2304]{1,0:T(8,128)(2,1)}, bf16[128,2304]{1,0:T(8,128)(2,1)}, u32[]{:S(2)}, u32[]{:S(2)}) %collective-permute-start.4) | collective-permute-done | bytes 589856 | tf_op jit(solution)/shard_map/ppermute | solution.py:12
  169.6 13.7 %conditional.11 = (f32[2304]{0:T(1024)S(1)}, bf16[3,128,1024]{2,1,0:T(8,128)(2,1)}, bf16[384,2304]{1,0:T(8,128)(2,1)}) conditional(s32[]{:T(128)} %convert_element_type.126, (f32[2304]{0:T(1024)S(1)}, bf16[3,128,1024]{2,1,0:T(8,128)(2,1)}, bf16[3,128,2304]{2,1,0:T(8,128)(2,1)}) %tuple.110, (bf16[3,128,2304]{2,1,0:T(8,128)(2,1)}, ...), branch_computations={%region_26.27_spmd, %region_27.30_spmd.clone.clone} | conditional | flops 1210744960 | bytes 16162016 | solution.py:92
  169.6 4.5 %bitcast_dynamic-update-slice_fusion.1 = (bf16[3,128,1024]{2,1,0:T(8,128)(2,1)}, bf16[128,1024]{1,0:T(8,128)(2,1)}) fusion(bf16[3,128,1024]{2,1,0:T(8,128)(2,1)} %get-tuple-element.456, s32[]{:T(128)S(6)} %select_n.156, bf16[2304,1024]{1,0:T(8,128)(2,1)} %get-tuple-element.453, pred[128,2304]{1,0:T(32,128)(4,1)} %get-tuple-element.449, ...), kind=kOutput, calls=%fused_computation.9 | convolution fusion | flops 604405760 | bytes 6717956 | tf_op jit(solution)/shard_map/cond/branch_1_fun/dot_general | solution.py:24
  176.9 4.1 %fusion = f32[2304]{0:T(1024)S(1)} fusion(bf16[128,1024]{1,0:T(8,128)(2,1)} %get-tuple-element.483, bf16[2304,1024]{1,0:T(8,128)(2,1)} %get-tuple-element.454, f32[128]{0:T(128)S(1)} %add_rsqrt_fusion, bf16[1,3,128,2304]{3,2,1,0:T(8,128)(2,1)S(1)} %get-tuple-element.455, s32[]{:T(128)S(6)} %select_n.155), kind=kOutput, calls=%fused_computation.4 | convolution fusion | flops 605157120 | bytes 5580292 | tf_op jit(solution)/shard_map/cond/branch_1_fun/dot_general | solution.py:25
  181.1 2.3 bitcast_dynamic-update-slice_fusion
  183.4 11.0 %fusion.56 = f32[2304,1024]{1,0:T(8,128)} fusion(bf16[384,2304]{1,0:T(8,128)(2,1)} %get-tuple-element.367, bf16[384,2304]{1,0:T(8,128)(2,1)S(1)} %bitcast.136, bf16[1,2304,1024]{2,1,0:T(8,128)(2,1)} %param.22), kind=kOutput, calls=%fused_computation.108 | convolution fusion | flops 3624271872 | bytes 17694720 | tf_op jit(solution)/shard_map/dot_general | solution.py:107
  194.4 7.1 %convolution_bitcast_fusion = f32[2304,1024]{1,0:T(8,128)} fusion(bf16[3,128,2304]{2,1,0:T(8,128)(2,1)S(1)} %copy-done.6, bf16[3,128,1024]{2,1,0:T(8,128)(2,1)} %get-tuple-element.357), kind=kOutput, calls=%fused_computation.100 | convolution fusion | flops 1811939328 | bytes 11993088 | tf_op jit(solution)/shard_map/dot_general | solution.py:104
  201.5 12.9 %psum.7 = f32[1,2304]{1,0:T(1,128)} all-reduce(f32[1,2304]{1,0:T(1,128)S(1)} %broadcast_in_dim.99), channel_id=1, replica_groups=mesh['section'=4,'seq'=8] {'seq'}, use_global_device_ids=true, to_apply=%region_32.33 | all-reduce | flops 2304 | bytes 18432 | tf_op jit(solution)/shard_map/psum | solution.py:114
  214.4 55.2 %reduce-scatter.5.cloned.1.call-done = f32[288,1024]{1,0:T(8,128)} async-done(((f32[2304,1024]{1,0:T(8,128)}), f32[288,1024]{1,0:T(8,128)}) %reduce-scatter.5.cloned.1.call-update) | async-done | bytes 1179664 | tf_op jit(solution)/shard_map/reduce_scatter | solution.py:112
  269.5 80.9 %reduce-scatter.3.cloned.1.call-done = f32[288,1024]{1,0:T(8,128)} async-done(((f32[2304,1024]{1,0:T(8,128)}), f32[288,1024]{1,0:T(8,128)}) %reduce-scatter.3.cloned.1.call-update) | async-done | bytes 1179664 | tf_op jit(solution)/shard_map/reduce_scatter | solution.py:111
  (65 shorter events, 16.3 us)
Async XLA Ops:
  7.2 262.4 %reduce-scatter.5.cloned.1.call-start = ((), (), s32[]{:S(2)}) async-start(), calls=%async_computation.3 | async-start | bytes 10616832 | tf_op jit(solution)/shard_map/reduce_scatter | solution.py:112
  20.6 21.5 %copy-start.1 = (bf16[3,128,2304]{2,1,0:T(8,128)(2,1)S(1)}, bf16[3,128,2304]{2,1,0:T(8,128)(2,1)}, u32[]{:S(2)}) copy-start(bf16[3,128,2304]{2,1,0:T(8,128)(2,1)} %param.19) | copy-start | bytes 5308420
  23.7 18.4 %collective-permute-start = (bf16[128,2304]{1,0:T(8,128)(2,1)}, bf16[128,2304]{1,0:T(8,128)(2,1)}, u32[]{:S(2)}, u32[]{:S(2)}) collective-permute-start(bf16[128,2304]{1,0:T(8,128)(2,1)} %get-tuple-element.337), channel_id=1, source_target_pairs={{8,0},{16,8},{24,16},{9,1},{17,9},{25,17},{10,2},{18,10},{26,18},{... | collective-permute-start | bytes 1769480 | tf_op jit(solution)/shard_map/ppermute | solution.py:12
  43.3 16.7 %collective-permute-start.1 = (bf16[128,2304]{1,0:T(8,128)(2,1)}, bf16[128,2304]{1,0:T(8,128)(2,1)}, u32[]{:S(2)}, u32[]{:S(2)}) collective-permute-start(bf16[128,2304]{1,0:T(8,128)(2,1)} %get-tuple-element.341), channel_id=1, source_target_pairs={{8,0},{16,8},{24,16},{9,1},{17,9},{25,17},{10,2},{18,10},{26,18},{... | collective-permute-start | bytes 1769480 | tf_op jit(solution)/shard_map/ppermute | solution.py:12
  61.1 2.7 copy-start.16
  61.1 49.9 %collective-permute-start.2 = (bf16[128,2304]{1,0:T(8,128)(2,1)}, bf16[128,2304]{1,0:T(8,128)(2,1)S(1)}, u32[]{:S(2)}, u32[]{:S(2)}) collective-permute-start(bf16[128,2304]{1,0:T(8,128)(2,1)} %get-tuple-element.345), channel_id=1, source_target_pairs={{8,0},{16,8},{24,16},{9,1},{17,9},{25,17},{10,2},{18,10},{26,18},{... | collective-permute-start | bytes 1769480 | tf_op jit(solution)/shard_map/ppermute | solution.py:12
  111.2 12.0 %copy-start.21 = (s32[3]{0:T(128)S(1)}, s32[3]{0:T(128)}, u32[]{:S(2)}) copy-start(s32[3]{0:T(128)} %fusion.57) | copy-start | bytes 40
  111.2 12.0 %copy-start = (bf16[1,3,128,2304]{3,2,1,0:T(8,128)(2,1)S(1)}, bf16[1,3,128,2304]{3,2,1,0:T(8,128)(2,1)}, u32[]{:S(2)}) copy-start(bf16[1,3,128,2304]{3,2,1,0:T(8,128)(2,1)} %param.18) | copy-start | bytes 5308420
  111.4 4.2 %copy-start.11 = (f32[1,2304]{1,0:T(1,128)S(1)}, f32[1,2304]{1,0:T(1,128)}, u32[]{:S(2)}) copy-start(f32[1,2304]{1,0:T(1,128)} %get-tuple-element.283) | copy-start | bytes 27652 | tf_op jit(solution)/shard_map/cond
  121.9 15.6 %collective-permute-start.3 = (bf16[128,2304]{1,0:T(8,128)(2,1)}, bf16[128,2304]{1,0:T(8,128)(2,1)}, u32[]{:S(2)}, u32[]{:S(2)}) collective-permute-start(bf16[128,2304]{1,0:T(8,128)(2,1)} %get-tuple-element.349), channel_id=1, source_target_pairs={{8,0},{16,8},{24,16},{9,1},{17,9},{25,17},{10,2},{18,10},{26,18},{... | collective-permute-start | bytes 1769480 | tf_op jit(solution)/shard_map/ppermute | solution.py:12
  140.6 4.2 %copy-start.7 = (bf16[128,2304]{1,0:T(8,128)(2,1)}, bf16[128,2304]{1,0:T(8,128)(2,1)S(1)}, u32[]{:S(2)}) copy-start(bf16[128,2304]{1,0:T(8,128)(2,1)S(1)} %get-tuple-element.481) | copy-start | bytes 1769476 | tf_op jit(solution)/shard_map/cond
  140.6 4.2 %copy-start.17 = (s32[1,3]{1,0:T(1,128)S(1)}, s32[1,3]{1,0:T(1,128)}, u32[]{:S(2)}) copy-start(s32[1,3]{1,0:T(1,128)} %get-tuple-element.435) | copy-start | bytes 40 | tf_op jit(solution)/shard_map/cond
  149.3 4.3 %copy-start.8 = (bf16[128,2304]{1,0:T(8,128)(2,1)S(1)}, bf16[128,2304]{1,0:T(8,128)(2,1)}, u32[]{:S(2)}) copy-start(bf16[128,2304]{1,0:T(8,128)(2,1)} %copy-done.7) | copy-start | bytes 1769476 | tf_op jit(solution)/shard_map/cond
  149.3 4.3 %copy-start.12 = (f32[2304]{0:T(1024)S(1)}, f32[2304]{0:T(1024)}, u32[]{:S(2)}) copy-start(f32[2304]{0:T(1024)} %reduce.5) | copy-start | bytes 27652 | tf_op jit(solution)/shard_map/cond
  149.3 4.3 %copy-start.19 = (f32[128]{0:T(128)S(1)}, f32[128]{0:T(128)}, u32[]{:S(2)}) copy-start(f32[128]{0:T(128)} %add_rsqrt_fusion.5) | copy-start | bytes 1540 | tf_op jit(solution)/shard_map/cond
  154.9 14.7 %collective-permute-start.4 = (bf16[128,2304]{1,0:T(8,128)(2,1)}, bf16[128,2304]{1,0:T(8,128)(2,1)}, u32[]{:S(2)}, u32[]{:S(2)}) collective-permute-start(bf16[128,2304]{1,0:T(8,128)(2,1)} %get-tuple-element.356), channel_id=1, source_target_pairs={{8,0},{16,8},{24,16},{9,1},{17,9},{25,17},{10,2},{18,10},{26,18},{... | collective-permute-start | bytes 1769480 | tf_op jit(solution)/shard_map/ppermute | solution.py:12
  169.6 13.7 %copy-start.6 = (bf16[3,128,2304]{2,1,0:T(8,128)(2,1)S(1)}, bf16[3,128,2304]{2,1,0:T(8,128)(2,1)}, u32[]{:S(2)}) copy-start(bf16[3,128,2304]{2,1,0:T(8,128)(2,1)} %fusion.55) | copy-start | bytes 5308420
  169.6 4.5 %copy-start.18 = (s32[1,3]{1,0:T(1,128)S(1)}, s32[1,3]{1,0:T(1,128)}, u32[]{:S(2)}) copy-start(s32[1,3]{1,0:T(1,128)} %get-tuple-element.458) | copy-start | bytes 40 | tf_op jit(solution)/shard_map/cond
  176.9 4.2 %copy-start.9 = (pred[128,2304]{1,0:T(32,128)(4,1)S(1)}, pred[128,2304]{1,0:T(32,128)(4,1)}, u32[]{:S(2)}) copy-start(pred[128,2304]{1,0:T(32,128)(4,1)} %get-tuple-element.449) | copy-start | bytes 884740 | tf_op jit(solution)/shard_map/cond
  194.3 156.1 %reduce-scatter.3.cloned.1.call-start = ((), (), s32[]{:S(2)}) async-start(), calls=%async_computation.2 | async-start | bytes 10616832 | tf_op jit(solution)/shard_map/reduce_scatter | solution.py:111
Sparse Core Ops, SparseCore 0:
  194.5 75.0 reduce-scatter.4
  273.6 76.8 reduce-scatter.2
where the time goes:
time: 358 us; the launch traced here: 357 us
  waiting for transfers between devices  238 us (66%)
  matrix products  43.2 us (12%)
  between operations  21.9 us (6%)
  other arithmetic  19.3 us (5%)
  blocking collectives  12.9 us (4%)
  local copies, waits for them, and re-layouts  11.3 us (3%)
  starting transfers between devices  6.5 us (2%)
  loops' own time  4.2 us (1%)
    ppermute x5, waiting for transfers between devices, passed_along(): lax.ppermute(value, axis, [(source, source + steps) for source in range(f...  102 us
    reduce_scatter x1, waiting for transfers between devices, per_device(): lax.psum_scatter(value_acc, 'seq', scatter_dimension=0, tiled=True)  80.9 us
    reduce_scatter x1, waiting for transfers between devices, per_device(): lax.psum_scatter(out_acc, 'seq', scatter_dimension=0, tiled=True)  55.2 us
    psum x1, blocking collectives, per_device(): gain_total = lax.psum(gain_acc, 'seq')  12.9 us
    dot_general x3, matrix products, input_grads(): lax.dot_general(grad_value, w_value, (((1,), (1,)), ((), ())), preferred_...  12.6 us
    dot_general x3, matrix products, input_grads(): jnp.dot(grad_out, w_out, preferred_element_type=jnp.float32)  12.6 us
    dot_general x1, matrix products, per_device(): lax.dot_general(grads_all, values_all, (((0,), (0,)), ((), ())), preferre...  11 us
  transfers between devices with their start and end apart: 7, of which 7 were waited for; matrix products, arithmetic and copies ran while one was open for 4% of the time, Pallas kernels for 0%

commit v1 on v0

--- a/solution.py
+++ b/solution.py
@@ -1,6 +1,10 @@
+import functools
+
 import jax
 import jax.numpy as jnp
 from jax import lax
+from jax.experimental import pallas as pl
+from jax.experimental.pallas import tpu as pltpu
 from jax.sharding import PartitionSpec as P
 
 EPSILON = 1e-06
@@ -115,6 +119,387 @@
     return (value_grad[None], out_grad[None], gain_total[None])
 
 
+TILE = 256
+LANES = 128
+VMEM_BYTES = 60 * 1024 * 1024
+
+
+def flipped(index, bits, count):
+    total, unit = 0, 1
+    while unit < count:
+        total = total + ((index // unit + (bits // unit) % 2) % 2) * unit
+        unit *= 2
+    return total
+
+
+def tile_at(index, size=TILE):
+    return pl.ds(pl.multiple_of(index * size, size), size)
+
+
+def fused_kernel(
+    peers,
+    sections,
+    slot_ref,
+    saved_ref,
+    cot_ref,
+    gain_ref,
+    wv_ref,
+    wo_ref,
+    vg_ref,
+    og_ref,
+    gg_ref,
+    inv_buf,
+    grad_buf,
+    pass_buf,
+    gn_buf,
+    rows_all,
+    turned,
+    cols_all,
+    gain_all,
+    rows_send,
+    rows_recv,
+    cols_send,
+    cols_recv,
+    down_send,
+    down_recv,
+    gain_send,
+    gain_recv,
+):
+    section = lax.axis_index("section")
+    me = lax.axis_index("seq")
+    micro, tokens, width = cot_ref.shape
+    inner = wv_ref.shape[1]
+    share = width // peers
+    wide, narrow = width // TILE, inner // TILE
+    top = section == sections - 1
+
+    def peer(bits):
+        return {"seq": flipped(me, bits, peers)}
+
+    def row_copy(kind, m, owner, sem, target):
+        place = rows_all.at[kind, m, tile_at(owner, tokens)]
+        return pltpu.make_async_remote_copy(
+            src_ref=place,
+            dst_ref=place,
+            send_sem=rows_send.at[kind, m, sem],
+            recv_sem=rows_recv.at[kind, m, sem],
+            device_id=target,
+            device_id_type=pl.DeviceIdType.MESH,
+        )
+
+    def own_rows(kind, m, bits):
+        return row_copy(kind, m, me, bits, peer(bits))
+
+    def relayed_rows(kind, m, bits):
+        return row_copy(kind, m, flipped(me, bits, peers), bits + 1, peer(1))
+
+    def arriving_rows(kind, m, bits):
+        return row_copy(kind, m, flipped(me, bits, peers), bits, peer(bits))
+
+    def col_copy(kind, m, owner, bits):
+        return pltpu.make_async_remote_copy(
+            src_ref=turned.at[kind, m, tile_at(flipped(me, bits, peers), share)],
+            dst_ref=cols_all.at[kind, m, :, tile_at(owner, tokens)],
+            send_sem=cols_send.at[kind, m, bits],
+            recv_sem=cols_recv.at[kind, m, bits],
+            device_id=peer(bits),
+            device_id_type=pl.DeviceIdType.MESH,
+        )
+
+    def down_copy(m, target):
+        return pltpu.make_async_remote_copy(
+            src_ref=pass_buf.at[m],
+            dst_ref=grad_buf.at[m],
+            send_sem=down_send.at[m],
+            recv_sem=down_recv.at[m],
+            device_id={"section": target},
+            device_id_type=pl.DeviceIdType.MESH,
+        )
+
+    def gain_copy(owner, bits):
+        return pltpu.make_async_remote_copy(
+            src_ref=gain_all.at[owner],
+            dst_ref=gain_all.at[owner],
+            send_sem=gain_send.at[bits],
+            recv_sem=gain_recv.at[bits],
+            device_id=peer(bits),
+            device_id_type=pl.DeviceIdType.MESH,
+        )
+
+    barrier = pltpu.get_barrier_semaphore()
+    for bits in range(1, peers):
+        pl.semaphore_signal(
+            barrier, inc=1, device_id=peer(bits), device_id_type=pl.DeviceIdType.MESH
+        )
+
+    @pl.when(section > 0)
+    def _():
+        pl.semaphore_signal(
+            barrier,
+            inc=1,
+            device_id={"section": section - 1},
+            device_id_type=pl.DeviceIdType.MESH,
+        )
+
+    @pl.when(section < sections - 1)
+    def _():
+        pl.semaphore_signal(
+            barrier,
+            inc=1,
+            device_id={"section": section + 1},
+            device_id_type=pl.DeviceIdType.MESH,
+        )
+
+    pl.semaphore_wait(
+        barrier,
+        peers - 1
+        + (section > 0).astype(jnp.int32)
+        + (section < sections - 1).astype(jnp.int32),
+    )
+
+    gain_all[me] = jnp.zeros((1, width), jnp.float32)
+    vg_ref[...] = jnp.zeros_like(vg_ref)
+    og_ref[...] = jnp.zeros_like(og_ref)
+
+    def scales(m, carry):
+        slot = slot_ref[0, m]
+
+        def squares(j, total):
+            x = saved_ref[slot, :, tile_at(j)].astype(jnp.float32)
+            return total + jnp.sum(x * x, axis=1, keepdims=True)
+
+        total = lax.fori_loop(0, wide, squares, jnp.zeros((tokens, 1), jnp.float32))
+        inv_buf[m] = lax.rsqrt(total / width + EPSILON)
+        return carry
+
+    lax.fori_loop(0, micro, scales, 0)
+
+    def send_cols(kind, m):
+        cols_all[kind, m, :, tile_at(me, tokens)] = turned[kind, m, tile_at(me, share)]
+        for bits in range(1, peers):
+            col_copy(kind, m, me, bits).start()
+
+    def send_rows(kind, m):
+        for bits in (*range(2, peers, 2), 1):
+            own_rows(kind, m, bits).start()
+
+    def values(m):
+        slot = slot_ref[0, m]
+        inv = inv_buf[m]
+
+        def norm(j, carry):
+            x = saved_ref[slot, :, tile_at(j)].astype(jnp.float32)
+            n = (x * inv * gain_ref[:, tile_at(j)]).astype(jnp.bfloat16)
+            pass_tile[:, tile_at(j)] = n
+            turned[0, m, tile_at(j)] = n.T
+            return carry
+
+        lax.fori_loop(0, wide, norm, 0)
+        send_cols(0, m)
+
+        def project(j, carry):
+            rows_all[0, m, tile_at(me, tokens), tile_at(j)] = jnp.dot(
+                pass_tile[...], wv_ref[:, tile_at(j)], preferred_element_type=jnp.float32
+            ).astype(jnp.bfloat16)
+            return carry
+
+        lax.fori_loop(0, narrow, project, 0)
+        send_rows(0, m)
+
+    pass_tile = gn_buf[0]
+    gn = gn_buf[1]
+
+    def chain(m):
+        slot = slot_ref[0, m]
+        inv = inv_buf[m]
+
+        @pl.when(top)
+        def _():
+            grad_buf[m] = cot_ref[m]
+
+        @pl.when(section < sections - 1)
+        def _():
+            down_copy(m, section + 1).wait_recv()
+
+        def project(j, carry):
+            rows_all[1, m, tile_at(me, tokens), tile_at(j)] = jnp.dot(
+                grad_buf[m], wo_ref[:, tile_at(j)], preferred_element_type=jnp.float32
+            ).astype(jnp.bfloat16)
+            return carry
+
+        lax.fori_loop(0, narrow, project, 0)
+        send_rows(1, m)
+
+        def back(j, total):
+            term = lax.dot_general(
+                rows_all[1, m, tile_at(me, tokens)],
+                wv_ref[tile_at(j)],
+                (((1,), (1,)), ((), ())),
+                preferred_element_type=jnp.float32,
+            )
+            unit = saved_ref[slot, :, tile_at(j)].astype(jnp.float32) * inv
+            gn[:, tile_at(j)] = term
+            both = term * unit
+            gain_all[me, :, tile_at(j)] += jnp.sum(both, axis=0, keepdims=True)
+            return total + jnp.sum(both * gain_ref[:, tile_at(j)], axis=1, keepdims=True)
+
+        total = lax.fori_loop(0, wide, back, jnp.zeros((tokens, 1), jnp.float32))
+        mean = total / width
+
+        @pl.when(section > 0)
+        def _():
+            def step(j, carry):
+                unit = saved_ref[slot, :, tile_at(j)].astype(jnp.float32) * inv
+                grad_unit = gn[:, tile_at(j)] * gain_ref[:, tile_at(j)]
+                pass_buf[m, :, tile_at(j)] = (
+                    grad_buf[m, :, tile_at(j)].astype(jnp.float32)
+                    + inv * (grad_unit - unit * mean)
+                ).astype(jnp.bfloat16)
+                return carry
+
+            lax.fori_loop(0, wide, step, 0)
+            down_copy(m, section - 1).start()
+
+        def turn(j, carry):
+            turned[1, m, tile_at(j)] = grad_buf[m, :, tile_at(j)].T
+            return carry
+
+        lax.fori_loop(0, wide, turn, 0)
+        send_cols(1, m)
+
+    def stage(t, carry):
+        at_top = top.astype(jnp.int32)
+        chained = at_top * (1 - t % 2) + (1 - at_top) * (t // micro)
+        m = at_top * (t // 2) + (1 - at_top) * (t % micro)
+
+        @pl.when(chained == 1)
+        def _():
+            chain(m)
+
+        @pl.when(chained == 0)
+        def _():
+            values(m)
+
+        return carry
+
+    lax.fori_loop(0, 2 * micro, stage, 0)
+    for bits in range(1, peers):
+        gain_copy(me, bits).start()
+
+    def finish(m, carry):
+        for kind in (0, 1):
+            for bits in range(2, peers, 2):
+                arriving_rows(kind, m, bits).wait_recv()
+                relayed_rows(kind, m, bits).start()
+        for kind in (0, 1):
+            for bits in range(1, peers):
+                col_copy(kind, m, flipped(me, bits, peers), bits).wait_recv()
+        for kind in (0, 1):
+            for bits in range(1, peers, 2):
+                arriving_rows(kind, m, bits).wait_recv()
+
+        def weight(j, inside):
+            vg_ref[:, tile_at(j)] += jnp.dot(
+                cols_all[0, m], rows_all[1, m, :, tile_at(j)], preferred_element_type=jnp.float32
+            )
+            og_ref[:, tile_at(j)] += jnp.dot(
+                cols_all[1, m], rows_all[0, m, :, tile_at(j)], preferred_element_type=jnp.float32
+            )
+            return inside
+
+        lax.fori_loop(0, narrow, weight, 0)
+        return carry
+
+    lax.fori_loop(0, micro, finish, 0)
+    for bits in range(1, peers):
+        gain_copy(flipped(me, bits, peers), bits).wait_recv()
+    gained = gain_all[0]
+    for owner in range(1, peers):
+        gained = gained + gain_all[owner]
+    gg_ref[...] = gained
+
+    def drain(m, carry):
+        for kind in (0, 1):
+            for bits in range(1, peers):
+                col_copy(kind, m, me, bits).wait_send()
+            for bits in (1, *range(2, peers, 2)):
+                own_rows(kind, m, bits).wait_send()
+            for bits in range(2, peers, 2):
+                relayed_rows(kind, m, bits).wait_send()
+
+        @pl.when(section > 0)
+        def _():
+            down_copy(m, section - 1).wait_send()
+
+        return carry
+
+    lax.fori_loop(0, micro, drain, 0)
+    for bits in range(1, peers):
+        gain_copy(me, bits).wait_send()
+
+
+def fused(mesh, saved, cotangent, slot_table, gain, value_weight, out_weight):
+    peers, sections = mesh.shape["seq"], mesh.shape["section"]
+    micro, tokens, width = cotangent.shape
+    inner = value_weight.shape[2]
+    share = width // peers
+    hbm = pl.BlockSpec(memory_space=pltpu.VMEM)
+    value_grad, out_grad, gain_grad = pl.pallas_call(
+        functools.partial(fused_kernel, peers, sections),
+        out_shape=(
+            jax.ShapeDtypeStruct((share, inner), jnp.float32),
+            jax.ShapeDtypeStruct((share, inner), jnp.float32),
+            jax.ShapeDtypeStruct((1, width), jnp.float32),
+        ),
+        in_specs=[pl.BlockSpec(memory_space=pltpu.SMEM)] + [hbm] * 5,
+        out_specs=(hbm, hbm, hbm),
+        scratch_shapes=[
+            pltpu.VMEM((micro, tokens, 1), jnp.float32),
+            pltpu.VMEM((micro, tokens, width), jnp.bfloat16),
+            pltpu.VMEM((micro, tokens, width), jnp.bfloat16),
+            (pltpu.VMEM((tokens, width), jnp.bfloat16), pltpu.VMEM((tokens, width), jnp.float32)),
+            pltpu.VMEM((2, micro, peers * tokens, inner), jnp.bfloat16),
+            pltpu.VMEM((2, micro, width, tokens), jnp.bfloat16),
+            pltpu.VMEM((2, micro, share, peers * tokens), jnp.bfloat16),
+            pltpu.VMEM((peers, 1, width), jnp.float32),
+            pltpu.SemaphoreType.DMA((2, micro, peers)),
+            pltpu.SemaphoreType.DMA((2, micro, peers)),
+            pltpu.SemaphoreType.DMA((2, micro, peers)),
+            pltpu.SemaphoreType.DMA((2, micro, peers)),
+            pltpu.SemaphoreType.DMA((micro,)),
+            pltpu.SemaphoreType.DMA((micro,)),
+            pltpu.SemaphoreType.DMA((peers,)),
+            pltpu.SemaphoreType.DMA((peers,)),
+        ],
+        compiler_params=pltpu.CompilerParams(
+            collective_id=0, has_side_effects=True, vmem_limit_bytes=VMEM_BYTES
+        ),
+    )(slot_table, saved[0], cotangent, gain, value_weight[0], out_weight[0])
+    return value_grad[None], out_grad[None], gain_grad
+
+
+def fits(mesh, saved, cotangent, slot_table, gain, value_weight, out_weight):
+    peers = mesh.shape["seq"]
+    micro, tokens, width = cotangent.shape
+    inner = value_weight.shape[2]
+    held = 4 * width * inner + 4 * micro * tokens * (2 * width + inner * peers)
+    held += 4 * micro * tokens * width * 3 + 8 * (width // peers) * inner + 6 * tokens * width
+    return (
+        peers & (peers - 1) == 0
+        and tokens % LANES == 0
+        and width % TILE == 0
+        and inner % TILE == 0
+        and width % (16 * peers) == 0
+        and held < VMEM_BYTES - 4 * 1024 * 1024
+    )
+
+
+def on_device(mesh, *arrays):
+    if fits(mesh, *arrays):
+        return fused(mesh, *arrays)
+    return per_device(*arrays)
+
+
 def solution(mesh):
     in_specs = (
         P("section", None, "seq", None),
@@ -126,5 +511,5 @@
     )
     out_specs = (P("section", "seq", None), P("section", "seq", None), P("section", None))
     return jax.shard_map(
-        per_device, mesh=mesh, in_specs=in_specs, out_specs=out_specs, check_vma=False
-    )
+        functools.partial(on_device, mesh), mesh=mesh, in_specs=in_specs, out_specs=out_specs, check_vma=False
+    )

time: 358 us -> 136 us (0.38)
  waiting for transfers between devices: 238 us -> 0 us
  Pallas kernels: 0 us -> 131 us
  matrix products: 43.2 us -> 0 us
  between operations: 21.9 us -> 0.65 us
  other arithmetic: 19.3 us -> 0 us
  blocking collectives: 12.9 us -> 0 us
  local copies, waits for them, and re-layouts: 11.3 us -> 4.12 us
  starting transfers between devices: 6.5 us -> 0 us
  loops' own time: 4.2 us -> 0 us
    reduce_scatter x2 -> x0, waiting for transfers between devices: 136 us -> none  [the longest x1 80.9 us: per_device(): lax.psum_scatter(value_acc, 'seq', scatter_dimension=0, tiled=True)]
    pallas_call x0 -> x1, Pallas kernels: none -> 131 us  [fused(): pl.pallas_call(functools.partial(fused_kernel, peers, sections), out_shap...]
    ppermute x5 -> x0, waiting for transfers between devices: 102 us -> none  [passed_along(): lax.ppermute(value, axis, [(source, source + steps) for source in range(f...]
    dot_general x8 -> x0, matrix products: 43.2 us -> none  [the longest x3 12.6 us: input_grads(): lax.dot_general(grad_value, w_value, (((1,), (1,)), ((), ())), preferred_...]
    psum x1 -> x0, blocking collectives: 12.9 us -> none  [per_device(): gain_total = lax.psum(gain_acc, 'seq')]
    ppermute x5 -> x0, starting transfers between devices: 6.42 us -> none  [passed_along(): lax.ppermute(value, axis, [(source, source + steps) for source in range(f...]
    convert_element_type x3 -> x0, other arithmetic: 5.06 us -> none  [the longest x2 2.54 us: input_grads(): return (grad_in.astype(jnp.bfloat16), grad_value, normed, gain_term)]
    dynamic_update_slice x2 -> x0, other arithmetic: 4.63 us -> none  [working(): new_out = lax.dynamic_update_index_in_dim(carried[2], grad_out, clipped, 0)]
  transfers between devices with their start and end apart: 7 -> 0, of which waited for: 7 -> 0; matrix products, arithmetic and copies ran while one was open for 4% -> 0% of each run, Pallas kernels for 0% -> 0%
where the time goes in v1:
time: 136 us
  Pallas kernels  131 us (96%)
  local copies, waits for them, and re-layouts  4.12 us (3%)
    pallas_call x1, Pallas kernels, fused(): pl.pallas_call(functools.partial(fused_kernel, peers, sections), out_shap...  131 us
    unnamed x7, local copies, waits for them, and re-layouts  4.12 us

profile of v1, /device:TPU:0, one launch (start us, length us, event | category | flops | bytes accessed | tf_op | source)
XLA Modules:
  0.0 135.8 jit_solution(6562707774510494726)
XLA Ops:
  0.6 131.0 %shard_map.85 = (f32[288,1024]{1,0:T(8,128)}, f32[288,1024]{1,0:T(8,128)}, f32[1,2304]{1,0:T(1,128)}) custom-call(s32[1,3]{1,0:T(1,128)} %slot_ref.1, bf16[3,128,2304]{2,1,0:T(8,128)(2,1)} %bitcast.7, bf16[3,128,2304]{2,1,0:T(8,128)(2,1)} %cot_ref.1, f32[1,2304]{1,0:T(1,128)} %gain_ref.1, bf16[2304,1024]{1,0:T(8,128)(2,1)} %bitcast.5, bf16[2304,1024]{1,0:T(8,128)(2,1)} %bitcast.6), custom_call_target="tpu_custom_call" | custom-call | tf_op jit(solution)/shard_map/pallas_call | solution.py:447
  131.6 0.0 copy-start
  131.6 2.5 %copy.12 = f32[1,288,1024]{2,1,0:T(8,128)} copy(f32[1,288,1024]{2,1,0:T(8,128)} %bitcast.9) | data formatting | bytes 2359296
  134.2 0.0 copy-done
  134.2 0.0 copy-start.1
  134.2 1.0 copy.13
  135.2 0.0 copy-done.1
  135.2 0.6 copy.14
Async XLA Ops:
  131.6 2.5 %copy-start = (f32[288,1024]{1,0:T(8,128)S(1)}, f32[288,1024]{1,0:T(8,128)}, u32[]{:S(2)}) copy-start(f32[288,1024]{1,0:T(8,128)} %get-tuple-element.7) | copy-start | bytes 3538948
  134.2 1.0 copy-start.1

commit v2 on v1

--- a/solution.py
+++ b/solution.py
@@ -120,6 +120,7 @@
 
 
 TILE = 256
+PIECES = 2
 LANES = 128
 VMEM_BYTES = 60 * 1024 * 1024
 
@@ -143,8 +144,8 @@
     saved_ref,
     cot_ref,
     gain_ref,
-    wv_ref,
-    wo_ref,
+    wv_hbm,
+    wo_hbm,
     vg_ref,
     og_ref,
     gg_ref,
@@ -164,7 +165,16 @@
     down_recv,
     gain_send,
     gain_recv,
+    wv_ref,
+    wo_ref,
+    load_sem,
 ):
+    loads = (
+        pltpu.make_async_copy(wo_hbm, wo_ref, load_sem.at[0]),
+        pltpu.make_async_copy(wv_hbm, wv_ref, load_sem.at[1]),
+    )
+    for load in loads:
+        load.start()
     section = lax.axis_index("section")
     me = lax.axis_index("seq")
     micro, tokens, width = cot_ref.shape
@@ -206,12 +216,14 @@
             device_id_type=pl.DeviceIdType.MESH,
         )
 
-    def down_copy(m, target):
+    piece = tokens // PIECES
+
+    def down_copy(m, h, target):
         return pltpu.make_async_remote_copy(
-            src_ref=pass_buf.at[m],
-            dst_ref=grad_buf.at[m],
-            send_sem=down_send.at[m],
-            recv_sem=down_recv.at[m],
+            src_ref=pass_buf.at[m, tile_at(h, piece)],
+            dst_ref=grad_buf.at[m, tile_at(h, piece)],
+            send_sem=down_send.at[m, h],
+            recv_sem=down_recv.at[m, h],
             device_id={"section": target},
             device_id_type=pl.DeviceIdType.MESH,
         )
@@ -273,6 +285,8 @@
         return carry
 
     lax.fori_loop(0, micro, scales, 0)
+    for load in loads:
+        load.wait()
 
     def send_cols(kind, m):
         cols_all[kind, m, :, tile_at(me, tokens)] = turned[kind, m, tile_at(me, share)]
@@ -311,54 +325,62 @@
 
     def chain(m):
         slot = slot_ref[0, m]
-        inv = inv_buf[m]
 
         @pl.when(top)
         def _():
             grad_buf[m] = cot_ref[m]
 
-        @pl.when(section < sections - 1)
-        def _():
-            down_copy(m, section + 1).wait_recv()
-
-        def project(j, carry):
-            rows_all[1, m, tile_at(me, tokens), tile_at(j)] = jnp.dot(
-                grad_buf[m], wo_ref[:, tile_at(j)], preferred_element_type=jnp.float32
-            ).astype(jnp.bfloat16)
-            return carry
-
-        lax.fori_loop(0, narrow, project, 0)
-        send_rows(1, m)
-
-        def back(j, total):
-            term = lax.dot_general(
-                rows_all[1, m, tile_at(me, tokens)],
-                wv_ref[tile_at(j)],
-                (((1,), (1,)), ((), ())),
-                preferred_element_type=jnp.float32,
-            )
-            unit = saved_ref[slot, :, tile_at(j)].astype(jnp.float32) * inv
-            gn[:, tile_at(j)] = term
-            both = term * unit
-            gain_all[me, :, tile_at(j)] += jnp.sum(both, axis=0, keepdims=True)
-            return total + jnp.sum(both * gain_ref[:, tile_at(j)], axis=1, keepdims=True)
-
-        total = lax.fori_loop(0, wide, back, jnp.zeros((tokens, 1), jnp.float32))
-        mean = total / width
-
-        @pl.when(section > 0)
-        def _():
-            def step(j, carry):
-                unit = saved_ref[slot, :, tile_at(j)].astype(jnp.float32) * inv
-                grad_unit = gn[:, tile_at(j)] * gain_ref[:, tile_at(j)]
-                pass_buf[m, :, tile_at(j)] = (
-                    grad_buf[m, :, tile_at(j)].astype(jnp.float32)
-                    + inv * (grad_unit - unit * mean)
+        def one_piece(h, done):
+            rows = tile_at(h, piece)
+            own = tile_at(me * PIECES + h, piece)
+            inv = inv_buf[m, rows]
+
+            @pl.when(section < sections - 1)
+            def _():
+                down_copy(m, h, section + 1).wait_recv()
+
+            def project(j, carry):
+                rows_all[1, m, own, tile_at(j)] = jnp.dot(
+                    grad_buf[m, rows], wo_ref[:, tile_at(j)], preferred_element_type=jnp.float32
                 ).astype(jnp.bfloat16)
                 return carry
 
-            lax.fori_loop(0, wide, step, 0)
-            down_copy(m, section - 1).start()
+            lax.fori_loop(0, narrow, project, 0)
+
+            def back(j, total):
+                term = lax.dot_general(
+                    rows_all[1, m, own],
+                    wv_ref[tile_at(j)],
+                    (((1,), (1,)), ((), ())),
+                    preferred_element_type=jnp.float32,
+                )
+                unit = saved_ref[slot, rows, tile_at(j)].astype(jnp.float32) * inv
+                gn[rows, tile_at(j)] = term
+                both = term * unit
+                gain_all[me, :, tile_at(j)] += jnp.sum(both, axis=0, keepdims=True)
+                return total + jnp.sum(both * gain_ref[:, tile_at(j)], axis=1, keepdims=True)
+
+            total = lax.fori_loop(0, wide, back, jnp.zeros((piece, 1), jnp.float32))
+            mean = total / width
+
+            @pl.when(section > 0)
+            def _():
+                def step(j, carry):
+                    unit = saved_ref[slot, rows, tile_at(j)].astype(jnp.float32) * inv
+                    grad_unit = gn[rows, tile_at(j)] * gain_ref[:, tile_at(j)]
+                    pass_buf[m, rows, tile_at(j)] = (
+                        grad_buf[m, rows, tile_at(j)].astype(jnp.float32)
+                        + inv * (grad_unit - unit * mean)
+                    ).astype(jnp.bfloat16)
+                    return carry
+
+                lax.fori_loop(0, wide, step, 0)
+                down_copy(m, h, section - 1).start()
+
+            return done
+
+        lax.fori_loop(0, PIECES, one_piece, 0)
+        send_rows(1, m)
 
         def turn(j, carry):
             turned[1, m, tile_at(j)] = grad_buf[m, :, tile_at(j)].T
@@ -429,7 +451,8 @@
 
         @pl.when(section > 0)
         def _():
-            down_copy(m, section - 1).wait_send()
+            for h in range(PIECES):
+                down_copy(m, h, section - 1).wait_send()
 
         return carry
 
@@ -443,7 +466,7 @@
     micro, tokens, width = cotangent.shape
     inner = value_weight.shape[2]
     share = width // peers
-    hbm = pl.BlockSpec(memory_space=pltpu.VMEM)
+    whole = pl.BlockSpec(memory_space=pltpu.VMEM)
     value_grad, out_grad, gain_grad = pl.pallas_call(
         functools.partial(fused_kernel, peers, sections),
         out_shape=(
@@ -451,8 +474,9 @@
             jax.ShapeDtypeStruct((share, inner), jnp.float32),
             jax.ShapeDtypeStruct((1, width), jnp.float32),
         ),
-        in_specs=[pl.BlockSpec(memory_space=pltpu.SMEM)] + [hbm] * 5,
-        out_specs=(hbm, hbm, hbm),
+        in_specs=[pl.BlockSpec(memory_space=pltpu.SMEM)] + [whole] * 3
+        + [pl.BlockSpec(memory_space=pl.ANY)] * 2,
+        out_specs=(whole, whole, whole),
         scratch_shapes=[
             pltpu.VMEM((micro, tokens, 1), jnp.float32),
             pltpu.VMEM((micro, tokens, width), jnp.bfloat16),
@@ -466,10 +490,13 @@
             pltpu.SemaphoreType.DMA((2, micro, peers)),
             pltpu.SemaphoreType.DMA((2, micro, peers)),
             pltpu.SemaphoreType.DMA((2, micro, peers)),
-            pltpu.SemaphoreType.DMA((micro,)),
-            pltpu.SemaphoreType.DMA((micro,)),
+            pltpu.SemaphoreType.DMA((micro, PIECES)),
+            pltpu.SemaphoreType.DMA((micro, PIECES)),
             pltpu.SemaphoreType.DMA((peers,)),
             pltpu.SemaphoreType.DMA((peers,)),
+            pltpu.VMEM((width, inner), jnp.bfloat16),
+            pltpu.VMEM((width, inner), jnp.bfloat16),
+            pltpu.SemaphoreType.DMA((2,)),
         ],
         compiler_params=pltpu.CompilerParams(
             collective_id=0, has_side_effects=True, vmem_limit_bytes=VMEM_BYTES

time: 136 us -> 139 us (1.022)
  the two profiles are of different devices: /device:TPU:0 before, /device:TPU:25 now
where the time goes in v2:
time: 139 us
  Pallas kernels  135 us (97%)
  local copies, waits for them, and re-layouts  4.12 us (3%)
    pallas_call x1, Pallas kernels, fused(): pl.pallas_call(functools.partial(fused_kernel, peers, sections), out_shap...  135 us
    unnamed x7, local copies, waits for them, and re-layouts  4.12 us

profile of v2, /device:TPU:25, one launch (start us, length us, event | category | flops | bytes accessed | tf_op | source)
XLA Modules:
  0.0 139.3 jit_solution(18049898437890759259)
XLA Ops:
  0.6 134.6 %shard_map.85 = (f32[288,1024]{1,0:T(8,128)}, f32[288,1024]{1,0:T(8,128)}, f32[1,2304]{1,0:T(1,128)}) custom-call(s32[1,3]{1,0:T(1,128)} %slot_ref.1, bf16[3,128,2304]{2,1,0:T(8,128)(2,1)} %bitcast.7, bf16[3,128,2304]{2,1,0:T(8,128)(2,1)} %cot_ref.1, f32[1,2304]{1,0:T(1,128)} %gain_ref.1, bf16[2304,1024]{1,0:T(8,128)(2,1)} %bitcast.5, bf16[2304,1024]{1,0:T(8,128)(2,1)} %bitcast.6), custom_call_target="tpu_custom_call" | custom-call | tf_op jit(solution)/shard_map/pallas_call | solution.py:470
  135.2 0.0 copy-start
  135.2 2.5 %copy.12 = f32[1,288,1024]{2,1,0:T(8,128)} copy(f32[1,288,1024]{2,1,0:T(8,128)} %bitcast.9) | data formatting | bytes 2359296
  137.7 0.0 copy-done
  137.7 0.0 copy-start.1
  137.7 1.0 copy.13
  138.7 0.0 copy-done.1
  138.7 0.6 copy.14
Async XLA Ops:
  135.2 2.5 %copy-start = (f32[288,1024]{1,0:T(8,128)S(1)}, f32[288,1024]{1,0:T(8,128)}, u32[]{:S(2)}) copy-start(f32[288,1024]{1,0:T(8,128)} %get-tuple-element.7) | copy-start | bytes 3538948
  137.7 1.0 copy-start.1
